TPU v7x, 256 devices: a whole 4x4x8 slice. The times are simulated.
256 devices in a mesh: grp: 16 (over y_lo, z), mem: 16 (over y_hi, x, core).
Axes of the slice: x: 4, y: 4 (y_hi: 2, y_lo: 2; y = y_hi * 2 + y_lo), z: 8, core: 2. Of those that a mesh axis runs over, the one named last changes fastest.
Arguments:
- client_input: bfloat16 [16, 16, 128, 896], P('grp', 'mem'), may hold values from -6 to 6
- client_gain: float32 [16, 896], P('mem'), may hold values from 0.5 to 1.5
- w_query: bfloat16 [16, 896, 896], P('mem'), may hold values from -1.5 to 1.5
- w_keyval: bfloat16 [16, 896, 256], P('mem'), may hold values from -0.5 to 0.5
- w_out: bfloat16 [16, 896, 896], P('mem'), may hold values from -0.1875 to 0.1875
- server_gain: float32 [16, 896], P('grp'), may hold values from 0.5 to 1.5
- w_gate: bfloat16 [16, 896, 4864], P('grp', None, 'mem'), may hold values from -0.1875 to 0.1875
- w_up: bfloat16 [16, 896, 4864], P('grp', None, 'mem'), may hold values from -0.1875 to 0.1875
- w_down: bfloat16 [16, 4864, 896], P('grp', 'mem'), may hold values from -0.078125 to 0.078125
- out_grad: bfloat16 [16, 16, 128, 896], P('grp', 'mem'), may hold values from -6 to 6
- valid: int32 [16, 16], P('grp', 'mem'), may hold values from 64 to 128
Outputs:
- server_out: bfloat16 [16, 16, 128, 896], P('grp', 'mem')
- grad_query: bfloat16 [16, 896, 896], P('mem')
- grad_keyval: bfloat16 [16, 896, 256], P('mem')
- grad_out: bfloat16 [16, 896, 896], P('mem')
- grad_gate: bfloat16 [16, 896, 4864], P('grp', None, 'mem')
- grad_up: bfloat16 [16, 896, 4864], P('grp', None, 'mem')
- grad_down: bfloat16 [16, 4864, 896], P('grp', 'mem')
All inputs are finite; a program needn't handle non-finite values.
Results may differ from a plain program's by a relative error of at most 0.03.
Values may be sent and summed in bfloat16 or wider, within the bound.
A program may use at most 128 MiB of HBM per device.

v0:
```python
import jax
import jax.numpy as jnp
from jax import lax
from jax.sharding import PartitionSpec as P

KV_HEADS = 2
HEAD_DIM = 64
EPS = 1e-06


def side_by_side(arrays, axis, dim, along):
    widths = [a.shape[along] for a in arrays]
    both = jnp.concatenate(arrays, axis=along)
    filled = lax.all_gather(both, axis, axis=dim, tiled=True)
    return tuple(jnp.split(filled, [sum(widths[:k]) for k in range(1, len(widths))], axis=along))


def gathered_total(shard, axis):
    return lax.all_gather(shard, axis).astype(jnp.float32).sum(0)


def client_forward(tokens_in, gain_vec, query_w, keyval_w, output_w):
    x_float = tokens_in.astype(jnp.float32)
    inv_rms = lax.rsqrt(jnp.mean(x_float * x_float, axis=-1, keepdims=True) + EPS)
    normed = (x_float * inv_rms * gain_vec).astype(jnp.bfloat16)
    queries = jnp.dot(normed, query_w, preferred_element_type=jnp.float32).astype(jnp.bfloat16)
    key_vals = jnp.dot(normed, keyval_w, preferred_element_type=jnp.float32).astype(jnp.bfloat16)
    length = tokens_in.shape[0]
    half_cols = KV_HEADS * HEAD_DIM
    q_heads = queries.reshape(length, KV_HEADS, -1, HEAD_DIM)
    k_heads = key_vals[:, :half_cols].reshape(length, KV_HEADS, HEAD_DIM)
    v_heads = key_vals[:, half_cols:].reshape(length, KV_HEADS, HEAD_DIM)
    scores = jnp.einsum(
        "tgqd,sgd->gqts", q_heads, k_heads, preferred_element_type=jnp.float32
    ) * HEAD_DIM ** (-0.5)
    causal = jnp.arange(length)[:, None] >= jnp.arange(length)[None, :]
    scores = jnp.where(causal, scores, -1e30)
    highest = jnp.max(scores, axis=-1, keepdims=True)
    expo = jnp.exp(scores - highest)
    probs = (expo / jnp.sum(expo, axis=-1, keepdims=True)).astype(jnp.bfloat16)
    attended = jnp.einsum("gqts,sgd->tgqd", probs, v_heads, preferred_element_type=jnp.float32)
    attended = attended.astype(jnp.bfloat16).reshape(length, -1)
    mixed = jnp.dot(attended, output_w, preferred_element_type=jnp.float32)
    return (x_float + mixed).astype(jnp.bfloat16)


def norm_back(h_float, inv_rms, gain_vec, upstream):
    scaled = upstream * gain_vec
    return inv_rms * scaled - h_float * inv_rms**3 * jnp.mean(
        scaled * h_float, axis=-1, keepdims=True
    )


def on_device(
    client_input,
    client_gain,
    w_query,
    w_keyval,
    w_out,
    server_gain,
    w_gate,
    w_up,
    w_down,
    out_grad,
    valid,
):
    tokens_in = client_input[0, 0]
    gain_vec = client_gain[0]
    query_w = w_query[0]
    keyval_w = w_keyval[0]
    output_w = w_out[0]
    s_gain = server_gain[0]
    gate_w = w_gate[0]
    up_w = w_up[0]
    down_w = w_down[0]
    length = tokens_in.shape[0]
    width = tokens_in.shape[1]
    contract_last = (((1,), (1,)), ((), ()))
    contract_first = (((0,), (0,)), ((), ()))

    def client_part(query_in, keyval_in, output_in):
        return client_forward(tokens_in, gain_vec, query_in, keyval_in, output_in)

    own_cut, pull = jax.vjp(client_part, query_w, keyval_w, output_w)
    live = jnp.arange(length) < valid[0, 0]
    own_cot = jnp.where(live[:, None], out_grad[0, 0], jnp.zeros_like(out_grad[0, 0]))
    all_cut, all_cot = side_by_side((own_cut, own_cot), "mem", 0, 1)
    h_float = all_cut.astype(jnp.float32)
    inv_rms = lax.rsqrt(jnp.mean(h_float * h_float, axis=-1, keepdims=True) + EPS)
    normed = (h_float * inv_rms * s_gain).astype(jnp.bfloat16)
    gate_act = jnp.dot(normed, gate_w, preferred_element_type=jnp.float32)
    up_act = jnp.dot(normed, up_w, preferred_element_type=jnp.float32)
    sigma = jax.nn.sigmoid(gate_act)
    hidden = (gate_act * sigma * up_act).astype(jnp.bfloat16)
    served = lax.psum_scatter(
        jnp.dot(hidden, down_w, preferred_element_type=jnp.float32).astype(jnp.bfloat16),
        "mem",
        scatter_dimension=0,
        tiled=True,
    ).astype(jnp.float32)
    own_float = own_cut.astype(jnp.float32)
    server_out = (own_float + served).astype(jnp.bfloat16)
    d_hidden = lax.dot_general(all_cot, down_w, contract_last, preferred_element_type=jnp.float32)
    d_gate = (d_hidden * up_act * sigma * (1.0 + gate_act * (1.0 - sigma))).astype(jnp.bfloat16)
    d_up = (d_hidden * gate_act * sigma).astype(jnp.bfloat16)
    grad_down = lax.dot_general(
        hidden, all_cot, contract_first, preferred_element_type=jnp.float32
    ).astype(jnp.bfloat16)
    grad_gate = lax.dot_general(
        normed, d_gate, contract_first, preferred_element_type=jnp.float32
    ).astype(jnp.bfloat16)
    grad_up = lax.dot_general(
        normed, d_up, contract_first, preferred_element_type=jnp.float32
    ).astype(jnp.bfloat16)
    d_normed = lax.dot_general(d_gate, gate_w, contract_last, preferred_element_type=jnp.float32)
    d_normed = d_normed + lax.dot_general(
        d_up, up_w, contract_last, preferred_element_type=jnp.float32
    )
    pushed = norm_back(h_float, inv_rms, s_gain, d_normed)
    local_sum = jnp.sum(pushed.reshape(-1, length, width), axis=0) + own_cot.astype(jnp.float32)
    grad_total = gathered_total(local_sum.astype(jnp.bfloat16), "mem").astype(jnp.float32)
    cut_grad = (grad_total / lax.axis_size("mem")).astype(jnp.bfloat16)
    grad_q, grad_kv, grad_o = pull(cut_grad)
    summed = (
        lax.psum(grad_q.astype(jnp.float32).astype(jnp.bfloat16), "grp").astype(jnp.float32),
        lax.psum(grad_kv.astype(jnp.float32).astype(jnp.bfloat16), "grp").astype(jnp.float32),
        lax.psum(grad_o.astype(jnp.float32).astype(jnp.bfloat16), "grp").astype(jnp.float32),
    )
    groups = lax.axis_size("grp")
    grad_query = (summed[0] / groups).astype(jnp.bfloat16)
    grad_keyval = (summed[1] / groups).astype(jnp.bfloat16)
    grad_out = (summed[2] / groups).astype(jnp.bfloat16)
    return (
        server_out[None, None],
        grad_query[None],
        grad_keyval[None],
        grad_out[None],
        grad_gate[None],
        grad_up[None],
        grad_down[None],
    )


def solution(mesh):
    in_specs = (
        P("grp", "mem", None, None),
        P("mem", None),
        P("mem", None, None),
        P("mem", None, None),
        P("mem", None, None),
        P("grp", None),
        P("grp", None, "mem"),
        P("grp", None, "mem"),
        P("grp", "mem", None),
        P("grp", "mem", None, None),
        P("grp", "mem"),
    )
    out_specs = (
        P("grp", "mem", None, None),
        P("mem", None, None),
        P("mem", None, None),
        P("mem", None, None),
        P("grp", None, "mem"),
        P("grp", None, "mem"),
        P("grp", "mem", None),
    )
    return jax.shard_map(
        on_device, mesh=mesh, in_specs=in_specs, out_specs=out_specs, check_vma=False
    )
```

profile of v0, /device:TPU:2, one launch (start us, length us, event | category | flops | bytes accessed | tf_op | source)
XLA Modules:
  0.0 434.7 jit_solution(6634465796072064970)
XLA Ops:
  8.0 1.1 fusion.63
  9.1 0.7 reduce
  9.8 1.4 convolution_convert_fusion.9
  11.5 2.1 fusion.29
  13.8 0.3 fusion.51
  14.1 0.3 copy-done.9
  15.2 0.5 fusion.35
  15.7 0.7 copy-done.7
  16.4 0.8 pad_maximum_fusion
  17.2 0.2 all-gather.5.cloned.1.call-start
  17.4 75.3 %all-gather.3.cloned.1.call-done = bf16[2048,1792]{1,0:T(8,128)(2,1)} async-done(((bf16[128,1792]{1,0:T(8,128)(2,1)}), bf16[2048,1792]{1,0:T(8,128)(2,1)}) %all-gather.3.cloned.1.call-update) | async-done | bytes 7340048 | tf_op jit(solution)/shard_map/all_gather | solution.py:14
  92.7 2.8 fusion
  95.6 2.6 fusion.2
  98.3 1.5 fusion.57
  99.8 0.3 copy-done.4
  100.1 1.5 fusion.61
  101.6 0.3 slice-done
  101.9 1.1 slice-done.1
  103.0 3.5 multiply_convert_fusion.2
  106.5 2.3 fusion.59
  108.8 3.4 fusion.5
  112.2 3.8 fusion.4
  116.0 4.2 reduce_sum.95
  120.2 1.9 fusion.69
  122.1 0.3 reduce-scatter.2.cloned.1.call-start
  122.4 5.6 %convolution_convert_fusion = bf16[2048,896]{1,0:T(8,128)(2,1)} fusion(bf16[2048,304]{0,1:T(8,128)(2,1)} %get-tuple-element.14, bf16[1,304,896]{2,1,0:T(8,128)(2,1)} %param.19), kind=kOutput, calls=%fused_computation.12 | convolution fusion | flops 1117519872 | bytes 5459968 | tf_op jit(solution)/shard_map/dot_general | solution.py:96
  128.1 0.6 multiply_divide_fusion
  128.7 51.6 %all-gather.5.cloned.1.call-done = bf16[16,128,896]{2,1,0:T(8,128)(2,1)} async-done(((bf16[1,128,896]{2,1,0:T(8,128)(2,1)}), bf16[16,128,896]{2,1,0:T(8,128)(2,1)}) %all-gather.5.cloned.1.call-update) | async-done | bytes 3670032 | tf_op jit(solution)/shard_map/all_gather | solution.py:19
  180.3 2.6 convert_reduce_fusion
  182.9 0.8 copy-done.2
  183.6 1.3 fusion.32
  184.9 1.8 copy.37
  186.7 1.4 fusion.47
  188.1 0.4 fusion.50
  188.6 0.4 fusion.45
  189.1 0.3 fusion.39
  189.4 0.3 fusion.38
  189.7 1.2 convolution_convert_fusion.5
  191.1 1.8 convolution_convert_fusion.2
  192.9 1.7 convolution_convert_fusion.1
  194.7 5.1 %fusion.22 = bf16[1,896,304]{1,2,0:T(8,128)(2,1)} fusion(bf16[2048,304]{0,1:T(8,128)(2,1)} %copy-done.11, bf16[2048,896]{1,0:T(8,128)(2,1)} %copy-done.4), kind=kOutput, calls=%fused_computation.43 | convolution fusion | flops 1115957248 | bytes 5459968 | tf_op jit(solution)/shard_map/dot_general | solution.py:112
  199.7 4.6 %fusion.21 = bf16[1,896,304]{1,2,0:T(8,128)(2,1)} fusion(bf16[2048,304]{0,1:T(8,128)(2,1)S(1)} %copy-done.6, bf16[2048,896]{1,0:T(8,128)(2,1)} %copy-done.4), kind=kOutput, calls=%fused_computation.42 | convolution fusion | flops 1115957248 | bytes 5459968 | tf_op jit(solution)/shard_map/dot_general | solution.py:109
  204.4 2.3 fusion.23
  206.6 62.0 %reduce-scatter.2.cloned.1.call-done = bf16[128,896]{1,0:T(8,128)(2,1)} async-done(((bf16[2048,896]{1,0:T(8,128)(2,1)}), bf16[128,896]{1,0:T(8,128)(2,1)}) %reduce-scatter.2.cloned.1.call-update) | async-done | bytes 229392 | tf_op jit(solution)/shard_map/reduce_scatter | solution.py:95
  268.6 1.7 fusion.72
  270.3 151.8 %all-reduce.5.cloned.1.call-done = (bf16[896,896]{1,0:T(8,128)(2,1)}, bf16[896,256]{1,0:T(8,128)(2,1)}, bf16[896,896]{1,0:T(8,128)(2,1)}) async-done(((bf16[896,896]{1,0:T(8,128)(2,1)}, bf16[896,256]{1,0:T(8,128)(2,1)}, bf16[896,896]{1,0:T(8,128)(2,1)}), (bf16[896,896]{1,0:T(8,128)(2,1)}, bf16[896,256]{1,0:T(8,128)(2,1)}, bf16[896,896]{1,0:T(8,128)(2,1)})) %all-reduce.5.cloned.1.call-update) | async-done | bytes 3670032 | tf_op jit(solution)/shard_map/psum | solution.py:125
  422.2 1.9 fusion.68
  424.0 4.2 fusion.10
  (74 shorter events, 1.7 us)
Async XLA Ops:
  7.2 8.0 %copy-start = (bf16[1,896,896]{2,1,0:T(8,128)(2,1)S(1)}, bf16[1,896,896]{2,1,0:T(8,128)(2,1)}, u32[]{:S(2)}) copy-start(bf16[1,896,896]{2,1,0:T(8,128)(2,1)} %param.15) | copy-start | bytes 4816900
  7.2 85.5 %all-gather.3.cloned.1.call-start = ((), (), s32[]{:S(2)}) async-start(), calls=%async_computation.1 | async-start | bytes 7798784 | tf_op jit(solution)/shard_map/all_gather | solution.py:14
  9.1 4.7 %copy-start.18 = (f32[128]{0:T(128)}, f32[128]{0:T(128)S(1)}, u32[]{:S(2)}) copy-start(f32[128]{0:T(128)S(1)} %add_rsqrt_fusion.1) | copy-start | bytes 1540
  9.8 4.0 copy-start.16
  13.6 1.3 copy-start.13
  13.8 0.7 copy-start.9
  13.8 1.4 copy-start.1
  14.8 2.6 copy-start.20
  15.7 0.7 copy-start.7
  17.2 163.1 %all-gather.5.cloned.1.call-start = ((), (), s32[]{:S(2)}) async-start(), calls=%async_computation.3 | async-start | bytes 3899392 | tf_op jit(solution)/shard_map/all_gather | solution.py:19
  95.6 2.6 copy-start.15
  98.2 1.9 copy-start.4
  98.2 1.9 copy-start.14
  98.2 3.7 slice-start
  100.1 2.9 slice-start.1
  100.1 2.9 copy-start.21
  106.5 2.3 copy-start.5
  106.5 2.3 copy-start.11
  122.1 146.5 %reduce-scatter.2.cloned.1.call-start = ((), (), s32[]{:S(2)}) async-start(), calls=%async_computation.2 | async-start | bytes 3899392 | tf_op jit(solution)/shard_map/reduce_scatter | solution.py:95
  128.0 294.2 %all-reduce.5.cloned.1.call-start = ((), (), s32[]{:S(2)}) async-start(), calls=%async_computation.4 | async-start | bytes 7340032 | tf_op jit(solution)/shard_map/psum | solution.py:125
  182.9 0.8 copy-start.2
  186.7 2.4 copy-start.10
  188.1 1.3 copy-start.12
  188.1 1.6 copy-start.17
  188.1 1.6 copy-start.19
  189.0 3.9 copy-start.3
  194.6 5.1 %copy-start.6 = (bf16[2048,304]{0,1:T(8,128)(2,1)S(1)}, bf16[2048,304]{0,1:T(8,128)(2,1)}, u32[]{:S(2)}) copy-start(bf16[2048,304]{0,1:T(8,128)(2,1)} %copy-done.5) | copy-start | bytes 3735556
  194.7 9.7 %slice-start.2 = ((s8[7340032]{0:T(1024)(128)(4,1)}), s8[4194304]{0:T(1024)(128)(4,1)S(1)}, s32[]{:S(2)}) async-start(s8[7340032]{0:T(1024)(128)(4,1)} %bitcast.184), calls=%async_computation.7 | async-start | bytes 8388608
  199.7 4.6 %slice-start.3 = ((s8[7340032]{0:T(1024)(128)(4,1)}), s8[3145728]{0:T(1024)(128)(4,1)S(1)}, s32[]{:S(2)}) async-start(s8[7340032]{0:T(1024)(128)(4,1)} %bitcast.184), calls=%async_computation.8 | async-start | bytes 6291456
  199.7 4.6 %copy-start.22 = (bf16[2048,304]{0,1:T(8,128)(2,1)S(1)}, bf16[2048,304]{0,1:T(8,128)(2,1)}, u32[]{:S(2)}) copy-start(bf16[2048,304]{0,1:T(8,128)(2,1)} %get-tuple-element.14) | copy-start | bytes 3735556
  204.4 64.3 %copy-start.8 = (bf16[128,896]{1,0:T(8,128)(2,1)S(1)}, bf16[128,896]{1,0:T(8,128)(2,1)}, u32[]{:S(2)}) copy-start(bf16[128,896]{1,0:T(8,128)(2,1)} %copy-done.7) | copy-start | bytes 688132
Sparse Core Ops, SparseCore 0:
  17.3 75.3 all-gather.2
  122.2 57.9 all-gather.4
  184.6 83.9 reduce-scatter.1
  272.0 150.1 all-reduce.4
where the time goes:
time: 435 us
  waiting for transfers between devices  341 us (78%)
  matrix products  42.4 us (10%)
  other arithmetic  30.3 us (7%)
  between operations  15 us (3%)
  local copies, waits for them, and re-layouts  5.74 us (1%)
    psum x1, waiting for transfers between devices, on_device(): lax.psum(grad_q.astype(jnp.float32).astype(jnp.bfloat16), 'grp')  152 us
    all_gather x1, waiting for transfers between devices, side_by_side(): filled = lax.all_gather(both, axis, axis=dim, tiled=True)  75.3 us
    reduce_scatter x1, waiting for transfers between devices, on_device(): lax.psum_scatter(jnp.dot(hidden, down_w, preferred_element_type=jnp.float...  62 us
    all_gather x1, waiting for transfers between devices, gathered_total(): return lax.all_gather(shard, axis).astype(jnp.float32).sum(0)  51.6 us
  transfers between devices with their start and end apart: 4, of which 4 were waited for; matrix products, arithmetic and copies ran while one was open for 8% of the time, Pallas kernels for 0%

commit v1 on v0

--- a/solution.py
+++ b/solution.py
@@ -122,7 +122,9 @@
     cut_grad = (grad_total / lax.axis_size("mem")).astype(jnp.bfloat16)
     grad_q, grad_kv, grad_o = pull(cut_grad)
     summed = (
-        lax.psum(grad_q.astype(jnp.float32).astype(jnp.bfloat16), "grp").astype(jnp.float32),
+        jnp.sum(
+            lax.all_gather(grad_q.astype(jnp.float32).astype(jnp.bfloat16), "grp"), axis=0
+        ).astype(jnp.float32),
         lax.psum(grad_kv.astype(jnp.float32).astype(jnp.bfloat16), "grp").astype(jnp.float32),
         lax.psum(grad_o.astype(jnp.float32).astype(jnp.bfloat16), "grp").astype(jnp.float32),
     )

time: 435 us -> 709 us (1.63)
  waiting for transfers between devices: 341 us -> 603 us
  other arithmetic: 30.3 us -> 42.9 us
    all_gather x0 -> x1, waiting for transfers between devices: none -> 270 us  [on_device(): lax.all_gather(grad_q.astype(jnp.float32).astype(jnp.bfloat16), 'grp')]
    reduce_sum x0 -> x1, other arithmetic: none -> 13.4 us  [on_device(): jnp.sum(lax.all_gather(grad_q.astype(jnp.float32).astype(jnp.bfloat16), '...]
    psum x1, waiting for transfers between devices: 152 us -> 143 us  [on_device(): lax.psum(grad_kv.astype(jnp.float32).astype(jnp.bfloat16), 'grp')]
  transfers between devices with their start and end apart: 4 -> 5, of which waited for: 4 -> 5; matrix products, arithmetic and copies ran while one was open for 8% -> 5% of each run, Pallas kernels for 0% -> 0%
where the time goes in v1:
time: 709 us; the launch traced here: 708 us
  waiting for transfers between devices  603 us (85%)
  other arithmetic  42.9 us (6%)
  matrix products  42.4 us (6%)
  between operations  15.1 us (2%)
    all_gather x1, waiting for transfers between devices, on_device(): lax.all_gather(grad_q.astype(jnp.float32).astype(jnp.bfloat16), 'grp')  270 us
    psum x1, waiting for transfers between devices, on_device(): lax.psum(grad_kv.astype(jnp.float32).astype(jnp.bfloat16), 'grp')  143 us
    all_gather x1, waiting for transfers between devices, side_by_side(): filled = lax.all_gather(both, axis, axis=dim, tiled=True)  75.3 us
    reduce_scatter x1, waiting for transfers between devices, on_device(): lax.psum_scatter(jnp.dot(hidden, down_w, preferred_element_type=jnp.float...  63.3 us
    all_gather x1, waiting for transfers between devices, gathered_total(): return lax.all_gather(shard, axis).astype(jnp.float32).sum(0)  51.7 us
  transfers between devices with their start and end apart: 5, of which 5 were waited for; matrix products, arithmetic and copies ran while one was open for 5% of the time, Pallas kernels for 0%

profile of v1, /device:TPU:2, one launch (start us, length us, event | category | flops | bytes accessed | tf_op | source)
XLA Modules:
  0.0 708.1 jit_solution(8471848691490064042)
XLA Ops:
  8.0 1.1 fusion.63
  9.1 0.7 reduce.1
  9.8 1.4 convolution_convert_fusion.9
  11.5 2.1 fusion.29
  13.8 0.3 fusion.51
  14.7 0.7 copy-done.2
  15.6 0.5 fusion.35
  16.1 0.8 pad_maximum_fusion
  17.2 75.3 %all-gather.5.cloned.1.call-done = bf16[2048,1792]{1,0:T(8,128)(2,1)} async-done(((bf16[128,1792]{1,0:T(8,128)(2,1)}), bf16[2048,1792]{1,0:T(8,128)(2,1)}) %all-gather.5.cloned.1.call-update) | async-done | bytes 7340048 | tf_op jit(solution)/shard_map/all_gather | solution.py:14
  92.5 2.8 fusion
  95.3 2.6 fusion.2
  98.0 1.5 fusion.57
  99.5 0.3 copy-done.6
  99.9 1.5 fusion.61
  101.4 0.3 slice-done
  101.7 1.1 slice-done.1
  102.8 3.5 multiply_convert_fusion.2
  106.2 2.3 fusion.59
  108.5 3.4 fusion.5
  111.9 3.7 fusion.4
  115.6 3.5 reduce_sum.107
  119.1 1.8 fusion.69
  120.9 0.3 reduce-scatter.2.cloned.1.call-start
  121.2 5.5 convolution_convert_fusion
  126.7 0.6 multiply_divide_fusion
  127.4 51.7 %all-gather.7.cloned.1.call-done = bf16[16,128,896]{2,1,0:T(8,128)(2,1)} async-done(((bf16[1,128,896]{2,1,0:T(8,128)(2,1)}), bf16[16,128,896]{2,1,0:T(8,128)(2,1)}) %all-gather.7.cloned.1.call-update) | async-done | bytes 3670032 | tf_op jit(solution)/shard_map/all_gather | solution.py:19
  179.0 2.6 convert_reduce_fusion
  181.7 0.8 copy-done.4
  182.4 0.6 fusion.32
  183.3 1.3 fusion.47
  184.5 0.4 fusion.50
  185.0 0.4 fusion.45
  185.5 0.3 fusion.39
  185.8 1.2 fusion.38
  187.1 1.2 convolution_convert_fusion.5
  188.2 1.7 convolution_convert_fusion.1
  190.2 1.8 convolution_convert_fusion.2
  192.1 5.0 fusion.22
  197.1 4.6 fusion.21
  201.8 2.3 fusion.23
  204.1 63.3 %reduce-scatter.2.cloned.1.call-done = bf16[128,896]{1,0:T(8,128)(2,1)} async-done(((bf16[2048,896]{1,0:T(8,128)(2,1)}), bf16[128,896]{1,0:T(8,128)(2,1)}) %reduce-scatter.2.cloned.1.call-update) | async-done | bytes 229392 | tf_op jit(solution)/shard_map/reduce_scatter | solution.py:95
  267.4 1.7 fusion.72
  269.1 143.2 %all-reduce.5.cloned.1.call-done = (bf16[896,256]{1,0:T(8,128)(2,1)}, bf16[896,896]{1,0:T(8,128)(2,1)}) async-done(((bf16[896,256]{1,0:T(8,128)(2,1)}, bf16[896,896]{1,0:T(8,128)(2,1)}), (bf16[896,256]{1,0:T(8,128)(2,1)}, bf16[896,896]{1,0:T(8,128)(2,1)})) %all-reduce.5.cloned.1.call-update) | async-done | bytes 2064400 | tf_op jit(solution)/shard_map/psum | solution.py:128
  412.3 1.9 fusion.68
  414.1 2.9 fusion.11
  417.0 269.7 %all-gather.9.cloned.1.call-done = bf16[14336,896]{1,0:T(8,128)(2,1)} async-done(((bf16[896,896]{1,0:T(8,128)(2,1)}), bf16[14336,896]{1,0:T(8,128)(2,1)}) %all-gather.9.cloned.1.call-update) | async-done | bytes 25690128 | tf_op jit(solution)/shard_map/all_gather | solution.py:126
  686.7 13.4 %reduce_sum.113 = bf16[896,896]{1,0:T(8,128)(2,1)S(1)} reduce(bf16[16,896,896]{2,1,0:T(8,128)(2,1)} %bitcast.188, bf16[]{:T(256)} %constant.32.clone.1), dimensions={0}, to_apply=%region_11.12 | reduce | flops 12042240 | bytes 27295746 | tf_op jit(solution)/shard_map/reduce_sum | solution.py:125
  700.1 1.4 fusion.10
  (87 shorter events, 2.2 us)
Async XLA Ops:
  7.2 8.4 %copy-start = (bf16[1,896,896]{2,1,0:T(8,128)(2,1)S(1)}, bf16[1,896,896]{2,1,0:T(8,128)(2,1)}, u32[]{:S(2)}) copy-start(bf16[1,896,896]{2,1,0:T(8,128)(2,1)} %param.15) | copy-start | bytes 4816900
  7.2 85.3 %all-gather.5.cloned.1.call-start = ((), (), s32[]{:S(2)}) async-start(), calls=%async_computation.1 | async-start | bytes 7798784 | tf_op jit(solution)/shard_map/all_gather | solution.py:14
  9.1 4.7 copy-start.21
  9.8 4.0 copy-start.18
  11.2 3.3 copy-start.15
  11.5 4.1 copy-start.1
  13.8 1.8 copy-start.11
  14.3 2.8 copy-start.24
  14.6 0.8 copy-start.2
  16.1 81.9 %copy-start.9 = (bf16[128,896]{1,0:T(8,128)(2,1)}, bf16[128,896]{1,0:T(8,128)(2,1)S(1)}, u32[]{:S(2)}) copy-start(bf16[128,896]{1,0:T(8,128)(2,1)S(1)} %fusion.35) | copy-start | bytes 688132
  16.9 162.1 %all-gather.7.cloned.1.call-start = ((), (), s32[]{:S(2)}) async-start(), calls=%async_computation.3 | async-start | bytes 3899392 | tf_op jit(solution)/shard_map/all_gather | solution.py:19
  95.3 2.7 copy-start.17
  98.0 1.9 copy-start.6
  98.0 1.9 copy-start.16
  98.0 3.7 slice-start
  99.8 2.9 slice-start.1
  99.9 2.9 copy-start.25
  106.2 2.3 copy-start.7
  106.2 2.3 copy-start.13
  120.9 146.5 %reduce-scatter.2.cloned.1.call-start = ((), (), s32[]{:S(2)}) async-start(), calls=%async_computation.2 | async-start | bytes 3899392 | tf_op jit(solution)/shard_map/reduce_scatter | solution.py:95
  126.7 285.6 %all-reduce.5.cloned.1.call-start = ((), (), s32[]{:S(2)}) async-start(), calls=%async_computation.5 | async-start | bytes 4128768 | tf_op jit(solution)/shard_map/psum | solution.py:128
  181.6 0.8 copy-start.4
  183.2 1.8 copy-start.14
  183.2 2.2 copy-start.12
  183.2 2.5 copy-start.3
  183.2 3.8 copy-start.19
  183.2 3.8 copy-start.22
  184.5 3.7 copy-start.5
  185.8 4.4 copy-start.20
  185.8 4.4 copy-start.23
  190.0 496.7 %all-gather.9.cloned.1.call-start = ((), (), s32[]{:S(2)}) async-start(), calls=%async_computation.4 | async-start | bytes 27295744 | tf_op jit(solution)/shard_map/all_gather | solution.py:126
  192.1 5.0 copy-start.8
  192.1 9.7 %slice-start.2 = ((s8[7340032]{0:T(1024)(128)(4,1)}), s8[4194304]{0:T(1024)(128)(4,1)S(1)}, s32[]{:S(2)}) async-start(s8[7340032]{0:T(1024)(128)(4,1)} %bitcast.185), calls=%async_computation.8 | async-start | bytes 8388608
  197.1 4.7 slice-start.3
  197.1 4.7 copy-start.26
  201.8 65.6 %copy-start.10 = (bf16[128,896]{1,0:T(8,128)(2,1)S(1)}, bf16[128,896]{1,0:T(8,128)(2,1)}, u32[]{:S(2)}) copy-start(bf16[128,896]{1,0:T(8,128)(2,1)} %copy-done.9) | copy-start | bytes 688132
Sparse Core Ops, SparseCore 0:
  17.0 75.3 all-gather.4
  121.0 57.9 all-gather.6
  183.4 83.9 reduce-scatter.1
  270.6 141.6 all-reduce.4
  414.5 272.1 all-gather.8
